TPU v7x, 32 devices: a whole 2x2x4 slice. The times are simulated.
32 devices in a mesh: section: 2 (over x), expert: 16 (over z, y, core).
Axes of the slice: x: 2, y: 2, z: 4, core: 2. Of those that a mesh axis runs over, the one named last changes fastest.
Arguments:
- images: bfloat16 [32, 256, 1408], P(('section', 'expert')), may hold values from -6 to 6
- norm_gain: bfloat16 [1408], replicated, may hold values from 0.5 to 1.5
- slot_map: bfloat16 [1408, 16], replicated, may hold values from -0.15625 to 0.15625
- logit_scale: float32 [1], replicated, may hold values from 30 to 80
- up_weight: bfloat16 [16, 5120, 1408], P('expert', 'section'), may hold values from -0.625 to 0.625
- down_weight: bfloat16 [16, 5120, 1408], P('expert', 'section'), may hold values from -0.3125 to 0.3125
Outputs:
- block_out: bfloat16 [32, 256, 1408], P(('section', 'expert'))
All inputs are finite; a program needn't handle non-finite values.
Results may differ from a plain program's by a relative error of at most 0.011.
Values may be sent and summed in bfloat16 or wider, within the bound.
A program may use at most 64 MiB of HBM per device.

v0:
```python
import functools

import jax
import jax.numpy as jnp
from jax import lax
from jax.experimental import pallas as pl
from jax.experimental.pallas import tpu as pltpu
from jax.sharding import PartitionSpec as P

epsilon = 1e-06
MESH = pl.DeviceIdType.MESH
NT = (((1,), (1,)), ((), ()))
TN = (((0,), (0,)), ((), ()))


def split_of(total, most, unit):
    best = unit
    for size in range(unit, most + 1, unit):
        if total % size == 0:
            best = size
    return best


def kernel(
    sections, experts, chunk,
    x_hbm, gain_ref, slot_ref, scale_ref, up_hbm, down_hbm,
    out_v,
    xs, normed, stat, up_v, down_v, send1, recv1, send2, recv2,
    x_sem, up_sem, down_sem, local_sem, send_sem, recv_sem,
):
    n = sections * experts
    tokens, width = xs.shape
    half = send1.shape[2]
    rest = width - half
    hidden_units = up_v.shape[0]
    chunks = hidden_units // chunk
    section = lax.axis_index("section")
    expert = lax.axis_index("expert")
    me = section * experts + expert

    x_parts = x_sem.shape[0]
    x_rows = tokens // x_parts
    x_copies = [
        pltpu.make_async_copy(
            x_hbm.at[pl.ds(i * x_rows, x_rows)], xs.at[pl.ds(i * x_rows, x_rows)], x_sem.at[i]
        )
        for i in range(x_parts)
    ]
    for copy in x_copies:
        copy.start()

    barrier = pltpu.get_barrier_semaphore()

    def wrapped(value, bound):
        return jnp.where(value >= bound, value - bound, value)

    def for_others(visit):
        def step(k, carry):
            s = wrapped(section + k // experts, sections)
            e = wrapped(expert + k % experts, experts)
            visit(s * experts + e, e, {"section": s, "expert": e})
            return carry

        if n <= 64:
            for k in range(n - 1, 0, -1):
                step(k, 0)
        else:
            lax.fori_loop(1, n, step, 0)

    def greet(target, e, device):
        pl.semaphore_signal(barrier, inc=1, device_id=device, device_id_type=MESH)

    for_others(greet)

    up_copies = []
    down_copies = []
    for c in range(chunks):
        rows = pl.ds(c * chunk, chunk)
        up_copies.append(pltpu.make_async_copy(up_hbm.at[rows], up_v.at[rows], up_sem.at[c]))
        down_copies.append(pltpu.make_async_copy(down_hbm.at[rows], down_v.at[rows], down_sem.at[c]))
    for copy in up_copies + down_copies:
        copy.start()

    columns = slot_ref[...].astype(jnp.float32)
    column_norm = jnp.sqrt(jnp.sum(columns * columns, axis=-1, keepdims=True) + epsilon)
    gain = gain_ref[...].astype(jnp.float32).reshape(1, width)

    step_rows = 16

    def norm_step(i, carry):
        rows = pl.ds(pl.multiple_of(i * step_rows, step_rows), step_rows)
        values = xs[rows, :].astype(jnp.float32)
        spread = jnp.sum(values * values, axis=-1, keepdims=True) * (1.0 / width)
        result = (values * lax.rsqrt(spread + epsilon) * gain).astype(jnp.bfloat16)
        normed[rows, :] = result
        wide = result.astype(jnp.float32)
        square = jnp.sum(wide * wide, axis=-1, keepdims=True)
        stat[rows, :] = jnp.broadcast_to(square, (step_rows, stat.shape[1]))
        return carry

    per = x_rows // step_rows
    for i, copy in enumerate(x_copies):
        copy.wait()
        lax.fori_loop(i * per, (i + 1) * per, norm_step, 0, unroll=True)

    raw = lax.dot_general(slot_ref[...], normed[...], NT, preferred_element_type=jnp.float32)
    token_norm = jnp.sqrt(jnp.transpose(stat[...])[0:1, :] + epsilon)
    logits = scale_ref[0] * raw / (token_norm * column_norm)
    scores = jnp.exp(logits)
    dispatch = (scores / jnp.sum(scores, axis=1, keepdims=True)).astype(jnp.bfloat16)
    combine = (scores / jnp.sum(scores, axis=0, keepdims=True)).astype(jnp.bfloat16)
    slot_in = jnp.dot(dispatch, normed[...], preferred_element_type=jnp.float32).astype(jnp.bfloat16)
    send1[:, 0, :] = slot_in[:, :half]
    send1[:, 1, :rest] = slot_in[:, half:]

    pl.semaphore_wait(barrier, n - 1)

    own1 = pltpu.make_async_copy(send1.at[expert], recv1.at[me], local_sem.at[0])
    own1.start()

    def dispatch_row(target, e, device):
        pltpu.make_async_remote_copy(
            src_ref=send1.at[e], dst_ref=recv1.at[me], send_sem=send_sem.at[0], recv_sem=recv_sem.at[0],
            device_id=device, device_id_type=MESH,
        ).start()

    for_others(dispatch_row)

    def wait_all(buffer, sem):
        part = buffer.at[pl.ds(0, n - 1)]
        pltpu.make_async_copy(part, part, sem).wait()

    own1.wait()
    wait_all(recv1, recv_sem.at[0])
    left = recv1[:, 0, :]
    right = recv1[:, 1, :rest]
    rows_in = jnp.concatenate([left, right], axis=1)
    total = None
    for c in range(chunks):
        rows = pl.ds(c * chunk, chunk)
        up_copies[c].wait()
        pre = lax.dot_general(rows_in, up_v[rows, :], NT, preferred_element_type=jnp.float32)
        act = jax.nn.gelu(pre).astype(jnp.bfloat16)
        down_copies[c].wait()
        term = jnp.dot(act, down_v[rows, :], preferred_element_type=jnp.float32)
        total = term if total is None else total + term
    partial = total.astype(jnp.bfloat16)
    send2[:, 0, :] = partial[:, :half]
    send2[:, 1, :rest] = partial[:, half:]

    own2 = pltpu.make_async_copy(send2.at[me], recv2.at[me], local_sem.at[1])
    own2.start()

    def return_row(target, e, device):
        pltpu.make_async_remote_copy(
            src_ref=send2.at[target], dst_ref=recv2.at[me], send_sem=send_sem.at[1], recv_sem=recv_sem.at[1],
            device_id=device, device_id_type=MESH,
        ).start()

    for_others(return_row)

    own2.wait()
    wait_all(recv2, recv_sem.at[1])
    summed = recv2[pl.ds(0, experts)].astype(jnp.float32)
    for s in range(1, sections):
        summed = summed + recv2[pl.ds(s * experts, experts)].astype(jnp.float32)
    slot_out = summed.astype(jnp.bfloat16)
    slot_out = jnp.concatenate([slot_out[:, 0, :], slot_out[:, 1, :rest]], axis=1)

    o_parts = 4
    o_rows = tokens // o_parts
    for i in range(o_parts):
        rows = pl.ds(i * o_rows, o_rows)
        mixed = lax.dot_general(
            combine[:, i * o_rows:(i + 1) * o_rows], slot_out, TN, preferred_element_type=jnp.float32
        )
        out_v[rows, :] = (xs[rows, :].astype(jnp.float32) + mixed).astype(jnp.bfloat16)
    wait_all(recv1, send_sem.at[0])
    wait_all(recv2, send_sem.at[1])


def solution(mesh):
    sections, experts = mesh.shape["section"], mesh.shape["expert"]
    n = sections * experts

    def local(images, norm_gain, slot_map, logit_scale, up_weight, down_weight):
        count, tokens, width = images.shape
        held, hidden_units, _ = up_weight.shape
        slots = slot_map.shape[1]
        assert count == 1 and held == 1 and slots == experts
        half = -(-width // 256) * 128
        chunk = split_of(hidden_units, 1280, 128)
        chunks = hidden_units // chunk
        bf16 = jnp.bfloat16
        hbm = pl.BlockSpec(memory_space=pl.ANY)
        vmem = pl.BlockSpec(memory_space=pltpu.VMEM)
        x_parts = 4
        result = pl.pallas_call(
            functools.partial(kernel, sections, experts, chunk),
            out_shape=pltpu.VMEM((tokens, width), bf16),
            in_specs=[hbm, vmem, vmem, pl.BlockSpec(memory_space=pltpu.SMEM), hbm, hbm],
            out_specs=vmem,
            scratch_shapes=[
                pltpu.VMEM((tokens, width), bf16),
                pltpu.VMEM((tokens, width), bf16),
                pltpu.VMEM((tokens, 128), jnp.float32),
                pltpu.VMEM((hidden_units, width), bf16),
                pltpu.VMEM((hidden_units, width), bf16),
                pltpu.VMEM((experts, 2, half), bf16),
                pltpu.VMEM((n, 2, half), bf16),
                pltpu.VMEM((n, 2, half), bf16),
                pltpu.VMEM((n, 2, half), bf16),
                pltpu.SemaphoreType.DMA((x_parts,)),
                pltpu.SemaphoreType.DMA((chunks,)),
                pltpu.SemaphoreType.DMA((chunks,)),
                pltpu.SemaphoreType.DMA((2,)),
                pltpu.SemaphoreType.DMA((2,)),
                pltpu.SemaphoreType.DMA((2,)),
            ],
            compiler_params=pltpu.CompilerParams(
                collective_id=0, has_side_effects=True, vmem_limit_bytes=60 * 1024 * 1024
            ),
        )(
            images.reshape(tokens, width), norm_gain, slot_map.T, logit_scale,
            up_weight.reshape(hidden_units, width), down_weight.reshape(hidden_units, width),
        )
        return result.reshape(1, tokens, width)

    return jax.shard_map(
        local,
        mesh=mesh,
        in_specs=(
            P(("section", "expert"), None, None),
            P(),
            P(),
            P(),
            P("expert", "section", None),
            P("expert", "section", None),
        ),
        out_specs=P(("section", "expert"), None, None),
        check_vma=False,
    )
```

profile of v0, /device:TPU:0, one launch (start us, length us, event | category | flops | bytes accessed | tf_op | source)
XLA Modules:
  0.0 23.7 jit_solution(17597890237698460756)
XLA Ops:
  0.7 22.1 %shard_map.64 = bf16[256,1408]{1,0:T(8,128)(2,1)S(1)} custom-call(bf16[256,1408]{1,0:T(8,128)(2,1)} %bitcast.8, bf16[1408]{0:T(1024)(128)(2,1)} %gain_ref.1, bf16[16,1408]{1,0:T(8,128)(2,1)} %bitcast.9, f32[1]{0:T(128)S(6)} %copy.9.scale_ref, bf16[2560,1408]{1,0:T(8,128)(2,1)} %bitcast.6, bf16[2560,1408]{1,0:T(8,128)(2,1)} %bitcast.7), custom_call_target="tpu_custom_call" | custom-call | tf_op jit(solution)/shard_map/pallas_call | solution.py:198
  22.8 0.9 %copy.8 = bf16[1,256,1408]{2,1,0:T(8,128)(2,1)} copy(bf16[1,256,1408]{2,1,0:T(8,128)(2,1)S(1)} %bitcast.5) | data formatting | bytes 1441792
where the time goes:
time: 23.9 us; the launch traced here: 23.7 us
  Pallas kernels  22.1 us (92%)
  local copies, waits for them, and re-layouts  0.86 us (4%)
  between operations  0.66 us (3%)
    pallas_call x1, Pallas kernels, local(): pl.pallas_call(functools.partial(kernel, sections, experts, chunk), out_s...  22.1 us
    unnamed x1, local copies, waits for them, and re-layouts  0.86 us

commit v1 on v0

--- a/solution.py
+++ b/solution.py
@@ -21,12 +21,20 @@
     return best
 
 
+def far_first(sections, experts):
+    def distance(k):
+        mask = k % experts
+        return -(k // experts + mask // 4 + mask // 2 % 2)
+
+    return sorted(range(1, sections * experts), key=distance)
+
+
 def kernel(
     sections, experts, chunk,
-    x_hbm, gain_ref, slot_ref, scale_ref, up_hbm, down_hbm,
+    x_hbm, gain_hbm, slot_hbm, scale_hbm, up_hbm, down_hbm,
     out_v,
-    xs, normed, stat, up_v, down_v, send1, recv1, send2, recv2,
-    x_sem, up_sem, down_sem, local_sem, send_sem, recv_sem,
+    gain_ref, slot_ref, scale_ref, xs, normed, stat, up_v, down_v, send1, recv1, send2, recv2,
+    small_sem, x_sem, up_sem, down_sem, local_sem, send_sem, recv_sem,
 ):
     n = sections * experts
     tokens, width = xs.shape
@@ -46,31 +54,51 @@
         )
         for i in range(x_parts)
     ]
-    for copy in x_copies:
-        copy.start()
+    small_copies = [
+        pltpu.make_async_copy(source, target, small_sem.at[i])
+        for i, (source, target) in enumerate(
+            [(gain_hbm, gain_ref), (slot_hbm, slot_ref), (scale_hbm, scale_ref)]
+        )
+    ]
 
     barrier = pltpu.get_barrier_semaphore()
 
     def wrapped(value, bound):
         return jnp.where(value >= bound, value - bound, value)
 
-    def for_others(visit):
-        def step(k, carry):
-            s = wrapped(section + k // experts, sections)
-            e = wrapped(expert + k % experts, experts)
-            visit(s * experts + e, e, {"section": s, "expert": e})
-            return carry
-
+    def visit_at(k, visit):
+        s = wrapped(section + k // experts, sections)
+        mask = k % experts
+        e = jnp.bitwise_xor(expert, mask) if paired else wrapped(expert + mask, experts)
+        visit(s * experts + e, e, {"section": s, "expert": e})
+
+    paired = experts & (experts - 1) == 0
+    order = far_first(sections, experts)
+
+    def for_others(visit, between=None):
         if n <= 64:
-            for k in range(n - 1, 0, -1):
-                step(k, 0)
+            for at, k in enumerate(order):
+                if at == 8 and between is not None:
+                    between()
+                visit_at(k, visit)
         else:
+            if between is not None:
+                between()
+
+            def step(k, carry):
+                visit_at(k, visit)
+                return carry
+
             lax.fori_loop(1, n, step, 0)
 
     def greet(target, e, device):
         pl.semaphore_signal(barrier, inc=1, device_id=device, device_id_type=MESH)
 
-    for_others(greet)
+    def start_inputs():
+        for copy in x_copies + small_copies:
+            copy.start()
+
+    for_others(greet, start_inputs)
 
     up_copies = []
     down_copies = []
@@ -81,6 +109,8 @@
     for copy in up_copies + down_copies:
         copy.start()
 
+    for copy in small_copies:
+        copy.wait()
     columns = slot_ref[...].astype(jnp.float32)
     column_norm = jnp.sqrt(jnp.sum(columns * columns, axis=-1, keepdims=True) + epsilon)
     gain = gain_ref[...].astype(jnp.float32).reshape(1, width)
@@ -198,9 +228,12 @@
         result = pl.pallas_call(
             functools.partial(kernel, sections, experts, chunk),
             out_shape=pltpu.VMEM((tokens, width), bf16),
-            in_specs=[hbm, vmem, vmem, pl.BlockSpec(memory_space=pltpu.SMEM), hbm, hbm],
+            in_specs=[hbm, hbm, hbm, pl.BlockSpec(memory_space=pltpu.HBM), hbm, hbm],
             out_specs=vmem,
             scratch_shapes=[
+                pltpu.VMEM((width,), bf16),
+                pltpu.VMEM((slots, width), bf16),
+                pltpu.SMEM((1,), jnp.float32),
                 pltpu.VMEM((tokens, width), bf16),
                 pltpu.VMEM((tokens, width), bf16),
                 pltpu.VMEM((tokens, 128), jnp.float32),
@@ -210,6 +243,7 @@
                 pltpu.VMEM((n, 2, half), bf16),
                 pltpu.VMEM((n, 2, half), bf16),
                 pltpu.VMEM((n, 2, half), bf16),
+                pltpu.SemaphoreType.DMA((3,)),
                 pltpu.SemaphoreType.DMA((x_parts,)),
                 pltpu.SemaphoreType.DMA((chunks,)),
                 pltpu.SemaphoreType.DMA((chunks,)),

time: 23.9 us -> 22.8 us (0.954)
  Pallas kernels: 22.1 us -> 21.1 us
    pallas_call x1, Pallas kernels: 22.1 us -> 21.1 us  [local(): pl.pallas_call(functools.partial(kernel, sections, experts, chunk), out_s...]
where the time goes in v1:
time: 22.8 us; the launch traced here: 22.6 us
  Pallas kernels  21.1 us (93%)
  local copies, waits for them, and re-layouts  0.86 us (4%)
  between operations  0.66 us (3%)
    pallas_call x1, Pallas kernels, local(): pl.pallas_call(functools.partial(kernel, sections, experts, chunk), out_s...  21.1 us
    unnamed x1, local copies, waits for them, and re-layouts  0.86 us

profile of v1, /device:TPU:0, one launch (start us, length us, event | category | flops | bytes accessed | tf_op | source)
XLA Modules:
  0.0 22.6 jit_solution(5206529917518700717)
XLA Ops:
  0.7 21.1 %shard_map.64 = bf16[256,1408]{1,0:T(8,128)(2,1)S(1)} custom-call(bf16[256,1408]{1,0:T(8,128)(2,1)} %bitcast.8, bf16[1408]{0:T(1024)(128)(2,1)} %gain_hbm.1, bf16[16,1408]{1,0:T(8,128)(2,1)} %bitcast.9, f32[1]{0:T(128)S(6)} %copy.9.scale_hbm, bf16[2560,1408]{1,0:T(8,128)(2,1)} %bitcast.6, bf16[2560,1408]{1,0:T(8,128)(2,1)} %bitcast.7), custom_call_target="tpu_custom_call" | custom-call | tf_op jit(solution)/shard_map/pallas_call | solution.py:228
  21.7 0.9 %copy.8 = bf16[1,256,1408]{2,1,0:T(8,128)(2,1)} copy(bf16[1,256,1408]{2,1,0:T(8,128)(2,1)S(1)} %bitcast.5) | data formatting | bytes 1441792

commit v2 on v1

--- a/solution.py
+++ b/solution.py
@@ -11,6 +11,8 @@
 MESH = pl.DeviceIdType.MESH
 NT = (((1,), (1,)), ((), ()))
 TN = (((0,), (0,)), ((), ()))
+U = 256
+STRIP = 16
 
 
 def split_of(total, most, unit):
@@ -29,7 +31,437 @@
     return sorted(range(1, sections * experts), key=distance)
 
 
-def kernel(
+def swap_pairs(v, even):
+    return jnp.where(even, pltpu.roll(v, v.shape[0] - 1, 0), pltpu.roll(v, 1, 0))
+
+def gelu(x):
+    k = 0.7978845608028654
+    return (0.5 * x) * (1.0 + jnp.tanh(x * (k + (k * 0.044715) * (x * x))))
+
+def expert_mlp(rows_ref, upt_v, down_v, act_v, out_ref, ups, downs, halves, half, width, lag=2):
+    M = rows_ref.shape[0]
+    hidden = upt_v.shape[1]
+    bf16 = jnp.bfloat16
+    right = width - half
+    blocks = hidden // U // 2
+    rem = right % U
+    tiles = [(0, j * U) for j in range(half // U)] + [(1, j * U) for j in range(right // U)]
+    tail = right // U * U
+    strips = M // STRIP
+    even = lax.broadcasted_iota(jnp.int32, (M, U), 0) % 2 == 0
+    even_strip = lax.broadcasted_iota(jnp.int32, (STRIP, U), 0) % 2 == 0
+    zero = jnp.zeros((M, U), bf16)
+    slot = [0, 0]
+
+    def piece(s):
+        return slice(s * STRIP, (s + 1) * STRIP)
+
+    def feed(q, tile, accs, operands):
+        r = slot[q]
+        slot[q] = 1 - r
+        pltpu.matmul_push_rhs(tile, r, q)
+        first = True
+        for acc, operand in zip(accs, operands):
+            for s in range(strips):
+                pltpu.matmul_acc_lhs(acc[s], operand[piece(s)], load_staged_rhs=r if first else None)
+                first = False
+
+    def at_block(q, b):
+        return pl.ds((q * blocks + b) * U, U)
+
+    lhs = []
+    for side, at in tiles:
+        v = rows_ref[:, at:at + U]
+        lhs.append(jnp.where(even, v, zero) if side == 0 else jnp.where(even, zero, v))
+    if rem:
+        v = rows_ref[:, tail:tail + rem]
+        v = jnp.where(even[:, :rem], zero[:, :rem], v)
+        lhs_tail = [jnp.concatenate([v, zero[:, :rem]], axis=1), jnp.concatenate([zero[:, :rem], v], axis=1)]
+
+    def finish(q, b, s):
+        pre = pltpu.matmul_pop(ups[q][b][s])
+        pre = pre + swap_pairs(pre, even_strip)
+        act_v[piece(s), at_block(q, b)] = gelu(pre).astype(bf16)
+
+    pending = []
+
+    def drain(count):
+        for _ in range(min(count, len(pending))):
+            pending.pop(0)()
+
+    def up_block(b, rate):
+        for side_at, operand in zip(tiles, lhs):
+            side, at = side_at
+            for q in range(2):
+                feed(q, upt_v[pl.ds(side * half + at, U), at_block(q, b)], [ups[q][b]], [operand])
+            drain(rate)
+        done = []
+        if rem:
+            k = pl.ds(half + tail, rem)
+            if b % 2 == 1:
+                for q in range(2):
+                    pair = jnp.concatenate([upt_v[k, at_block(q, b - 1)], upt_v[k, at_block(q, b)]], axis=0)
+                    feed(q, pair, [ups[q][b - 1], ups[q][b]], lhs_tail)
+                done = [b - 1, b]
+            elif b == blocks - 1:
+                for q in range(2):
+                    one = upt_v[k, at_block(q, b)]
+                    feed(q, jnp.concatenate([one, one], axis=0), [ups[q][b]], lhs_tail[:1])
+                done = [b]
+        else:
+            done = [b]
+        for d in done:
+            for s in range(strips):
+                for q in range(2):
+                    pending.append(lambda q=q, d=d, s=s: finish(q, d, s))
+
+    for b in range(blocks):
+        up_block(b, lag)
+
+    def act(q, b):
+        return act_v[:, at_block(q, b)]
+
+    def down_step(j, b):
+        side, at = tiles[j]
+        for q in range(2):
+            feed(q, down_v[at_block(q, b), pl.ds(side * half + at, U)], [downs[q][j]], [act(q, b)])
+
+    def down_tail(pair):
+        cols = pl.ds(half + tail, rem)
+        for q in range(2):
+            v = [down_v[at_block(q, b), cols] for b in pair]
+            if len(v) == 1:
+                v = v * 2
+            feed(q, jnp.concatenate(v, axis=1), [halves[q][i] for i in range(len(pair))], [act(q, b) for b in pair])
+
+    nl, nr = half // U, right // U
+    pairs = [list(range(b, min(b + 2, blocks))) for b in range(0, blocks, 2)]
+
+    def total(group, s):
+        return pltpu.matmul_pop(group[0][s]) + pltpu.matmul_pop(group[1][s])
+
+    def emit(j, s):
+        l = total([downs[0][j], downs[1][j]], s)
+        rows = piece(s)
+        if j < nr:
+            r = total([downs[0][nl + j], downs[1][nl + j]], s)
+            out_ref[rows, j * U:(j + 1) * U] = jnp.where(even_strip, l, r).astype(bf16)
+        elif rem:
+            r = total([halves[0][0], halves[1][0]], s)[:, :rem] + total([halves[0][1], halves[1][1]], s)[:, rem:]
+            both = jnp.where(even_strip[:, :rem], l[:, :rem], r)
+            out_ref[rows, j * U:(j + 1) * U] = jnp.concatenate([both, l[:, rem:]], axis=1).astype(bf16)
+        else:
+            out_ref[rows, j * U:(j + 1) * U] = l.astype(bf16)
+
+    ready = blocks - 1 if blocks % 2 else blocks - 2
+    groups = []
+    for j in reversed(range(nl)):
+        groups.append((j, [j] + ([nl + j] if j < nr else [])))
+    first = True
+    for j, columns in groups:
+        tails = rem and j >= nr
+        for b in range(blocks):
+            if first and b == ready:
+                drain(len(pending))
+            for c in columns:
+                down_step(c, b)
+                drain(lag)
+            if tails and (b % 2 == 1 or b == blocks - 1):
+                down_tail(pairs[b // 2])
+                drain(lag)
+        drain(len(pending))
+        first = False
+        for s in range(strips):
+            pending.append(lambda j=j, s=s: emit(j, s))
+    drain(len(pending))
+
+def routing_kernel(
+    sections, experts, half,
+    x_hbm, gain_hbm, slot_hbm, scale_ref, up_hbm, down_hbm,
+    xs, back, mix_left, mix_right,
+    gain_ref, slot_ref, normed, stat, up_v, upt_v, down_v, act_v, send1, recv1, send2, recv2, sized,
+    small_sem, x_sem, up_sem, down_sem, local_sem, send_sem, recv_sem,
+):
+    tokens, width = xs.shape
+    slots = slot_ref.shape[0]
+    padded = normed.shape[1]
+    columns = padded // U
+    images = sections * experts
+
+    def spec(rows):
+        return lambda q: [pltpu.ACC(q)((STRIP, U), jnp.float32) for _ in range(rows // STRIP)]
+
+    def per_unit(count, rows):
+        make = spec(rows)
+        return [[make(q) for _ in range(count)] for q in range(2)]
+
+    hidden = up_v.shape[0]
+    wide = half // U + (width - half) // U
+
+    def run(raws, ins, ups, downs, halves):
+        routing_body(
+            sections, experts, half,
+            x_hbm, gain_hbm, slot_hbm, scale_ref, up_hbm, down_hbm,
+            xs, back, mix_left, mix_right,
+            gain_ref, slot_ref, normed, stat, up_v, upt_v, down_v, act_v, send1, recv1, send2, recv2, sized,
+            small_sem, x_sem, up_sem, down_sem, local_sem, send_sem, recv_sem,
+            raws, ins, ups, downs, halves,
+        )
+
+    pl.run_scoped(
+        run,
+        [pltpu.ACC(q)((slots, U), jnp.float32) for q in range(2)],
+        [pltpu.ACC(t % 2)((2 * slots, U), jnp.float32) for t in range(columns)],
+        per_unit(hidden // U // 2, 2 * images),
+        per_unit(wide, 2 * images),
+        per_unit(2, 2 * images),
+    )
+
+
+def routing_body(
+    sections, experts, half,
+    x_hbm, gain_hbm, slot_hbm, scale_ref, up_hbm, down_hbm,
+    xs, back, mix_left, mix_right,
+    gain_ref, slot_ref, normed, stat, up_v, upt_v, down_v, act_v, send1, recv1, send2, recv2, sized,
+    small_sem, x_sem, up_sem, down_sem, local_sem, send_sem, recv_sem,
+    raws, ins, ups, downs, halves,
+):
+    n = sections * experts
+    tokens, width = xs.shape
+    slots = slot_ref.shape[0]
+    padded = normed.shape[1]
+    hidden = up_v.shape[0]
+    bf16 = jnp.bfloat16
+    section = lax.axis_index("section")
+    expert = lax.axis_index("expert")
+    me = section * experts + expert
+
+    x_parts = x_sem.shape[0]
+    x_rows = tokens // x_parts
+    x_copies = [
+        pltpu.make_async_copy(
+            x_hbm.at[pl.ds(i * x_rows, x_rows)], xs.at[pl.ds(i * x_rows, x_rows)], x_sem.at[i]
+        )
+        for i in range(x_parts)
+    ]
+    small_copies = [
+        pltpu.make_async_copy(gain_hbm, gain_ref, small_sem.at[0]),
+        pltpu.make_async_copy(slot_hbm, slot_ref, small_sem.at[1]),
+    ]
+
+    barrier = pltpu.get_barrier_semaphore()
+
+    def for_others(visit, between=None):
+        for at, k in enumerate(far_first(sections, experts)):
+            if at == 8 and between is not None:
+                between()
+            s = lax.rem(section + k // experts, sections)
+            e = jnp.bitwise_xor(expert, k % experts)
+            visit(s * experts + e, e, {"section": s, "expert": e})
+
+    def greet(target, e, device):
+        pl.semaphore_signal(barrier, inc=1, device_id=device, device_id_type=MESH)
+
+    def start_inputs():
+        for copy in x_copies + small_copies:
+            copy.start()
+
+    for_others(greet, start_inputs)
+
+    up_parts, down_parts = up_sem.shape[0], down_sem.shape[0]
+    up_rows, down_rows = hidden // up_parts, hidden // down_parts
+
+    def up_copy(c):
+        rows = pl.ds(pl.multiple_of(c * up_rows, up_rows), up_rows)
+        return pltpu.make_async_copy(up_hbm.at[rows], up_v.at[rows], up_sem.at[c])
+
+    def down_copy(c):
+        rows = pl.ds(c * down_rows, down_rows)
+        return pltpu.make_async_copy(down_hbm.at[rows], down_v.at[rows], down_sem.at[c])
+
+    for c in range(up_parts):
+        up_copy(c).start()
+    for c in range(down_parts):
+        down_copy(c).start()
+
+    for copy in small_copies:
+        copy.wait()
+    slot_rows = slot_ref[...]
+    slot_wide = slot_rows.astype(jnp.float32)
+    column_norm = jnp.sqrt(jnp.sum(slot_wide * slot_wide, axis=-1, keepdims=True) + epsilon)
+    gain = gain_ref[...].astype(jnp.float32).reshape(1, width)
+    if padded > width:
+        normed[:, width:] = jnp.zeros((tokens, padded - width), bf16)
+        slot_rows = jnp.concatenate([slot_rows, jnp.zeros((slots, padded - width), bf16)], axis=1)
+
+    step_rows = 16
+
+    def norm_step(i, carry):
+        rows = pl.ds(pl.multiple_of(i * step_rows, step_rows), step_rows)
+        values = xs[rows, :].astype(jnp.float32)
+        spread = jnp.sum(values * values, axis=-1, keepdims=True) * (1.0 / width)
+        result = (values * lax.rsqrt(spread + epsilon) * gain).astype(bf16)
+        normed[rows, :width] = result
+        wide = result.astype(jnp.float32)
+        square = jnp.sum(wide * wide, axis=-1, keepdims=True)
+        stat[rows, :] = jnp.broadcast_to(square, (step_rows, stat.shape[1]))
+        return carry
+
+    per = x_rows // step_rows
+    for i, copy in enumerate(x_copies):
+        copy.wait()
+        lax.fori_loop(i * per, (i + 1) * per, norm_step, 0, unroll=True)
+
+    tiles = padded // U
+    for t in range(tiles):
+        q, r = t % 2, t // 2 % 2
+        pltpu.matmul_push_rhs(normed[:, t * U:(t + 1) * U], r, q, transpose=True)
+        pltpu.matmul_acc_lhs(raws[q], slot_rows[:, t * U:(t + 1) * U], load_staged_rhs=r)
+    raw = pltpu.matmul_pop(raws[0]) + pltpu.matmul_pop(raws[1])
+    token_norm = jnp.sqrt(jnp.transpose(stat[...])[0:1, :] + epsilon)
+    logits = scale_ref[0] * raw / (token_norm * column_norm)
+    scores = jnp.exp(logits)
+    dispatch = scores / jnp.sum(scores, axis=1, keepdims=True)
+    combine = scores / jnp.sum(scores, axis=0, keepdims=True)
+    dispatch = jnp.repeat(dispatch, 2, axis=0).astype(bf16)
+    even = lax.broadcasted_iota(jnp.int32, (2 * slots, U), 0) % 2 == 0
+    shift = tiles // 2
+    for j in range(shift):
+        for t in (j, j + shift):
+            q, r = t % 2, t // 2 % 2
+            pltpu.matmul_push_rhs(normed[:, t * U:(t + 1) * U], r, q)
+            pltpu.matmul_acc_lhs(ins[t], dispatch, load_staged_rhs=r)
+    for j in range(shift):
+        left, right = pltpu.matmul_pop(ins[j]), pltpu.matmul_pop(ins[j + shift])
+        send1[:, j * U:(j + 1) * U] = jnp.where(even, left, right).astype(bf16)
+
+    pl.semaphore_wait(barrier, n - 1)
+
+    def pair(index):
+        return pl.ds(pl.multiple_of(2 * index, 2), 2)
+
+    def send_rows(source, target, i, by_expert):
+        def visit(index, e, device):
+            pltpu.make_async_remote_copy(
+                src_ref=source.at[pair(e if by_expert else index)], dst_ref=target.at[pair(me)],
+                send_sem=send_sem.at[i], recv_sem=recv_sem.at[i],
+                device_id=device, device_id_type=MESH,
+            ).start()
+
+        for_others(visit)
+
+    def wait_all(sem):
+        pltpu.make_async_copy(sized, sized, sem).wait()
+
+    send_rows(send1, recv1, 0, True)
+    own1 = pltpu.make_async_copy(send1.at[pair(expert)], recv1.at[pair(me)], local_sem.at[0])
+    own1.start()
+
+    stacked = jnp.concatenate([jnp.repeat(combine, 2, axis=0)] * sections, axis=0)
+    by_token = jnp.transpose(stacked)
+    lane_even = lax.broadcasted_iota(jnp.int32, by_token.shape, 1) % 2 == 0
+    mix_left[...] = jnp.where(lane_even, by_token, 0.0).astype(bf16)
+    mix_right[...] = jnp.where(lane_even, 0.0, by_token).astype(bf16)
+
+    def turn(c, carry):
+        up_copy(c).wait()
+        at = pl.multiple_of(c * up_rows, up_rows)
+        for k in range(0, width, 128):
+            upt_v[k:k + 128, pl.ds(at, up_rows)] = up_v[pl.ds(at, up_rows), k:k + 128].T
+        return carry
+
+    lax.fori_loop(0, up_parts, turn, 0)
+    for c in range(down_parts):
+        down_copy(c).wait()
+
+    own1.wait()
+    wait_all(recv_sem.at[0])
+    expert_mlp(recv1, upt_v, down_v, act_v, send2, ups, downs, halves, half, width)
+
+    send_rows(send2, recv2, 1, False)
+    own2 = pltpu.make_async_copy(send2.at[pair(me)], recv2.at[pair(me)], local_sem.at[1])
+    own2.start()
+    wait_all(send_sem.at[0])
+    own2.wait()
+    wait_all(recv_sem.at[1])
+    back[...] = recv2[...]
+    wait_all(send_sem.at[1])
+
+
+def mixing_kernel(half, xs, back, mix_left, mix_right, out_hbm, out_v, sem):
+    tokens, width = xs.shape
+    parts = sem.shape[0]
+    rows_each = tokens // parts
+    copies = []
+    for i in range(parts):
+        rows = pl.ds(i * rows_each, rows_each)
+        left = jnp.dot(mix_left[rows, :], back[...], preferred_element_type=jnp.float32)
+        right = jnp.dot(mix_right[rows, :], back[:, :width - half], preferred_element_type=jnp.float32)
+        out_v[rows, :half] = (xs[rows, :half].astype(jnp.float32) + left).astype(jnp.bfloat16)
+        out_v[rows, half:] = (xs[rows, half:].astype(jnp.float32) + right).astype(jnp.bfloat16)
+        copy = pltpu.make_async_copy(out_v.at[rows], out_hbm.at[rows], sem.at[i])
+        copy.start()
+        copies.append(copy)
+    for copy in copies:
+        copy.wait()
+
+
+def fast_call(sections, experts, half, images, norm_gain, slot_map, logit_scale, up_weight, down_weight):
+    tokens, width = images.shape
+    hidden = up_weight.shape[0]
+    slots = slot_map.shape[0]
+    n = sections * experts
+    padded = -(-width // (2 * U)) * 2 * U
+    bf16 = jnp.bfloat16
+    hbm = pl.BlockSpec(memory_space=pl.ANY)
+    vmem = pl.BlockSpec(memory_space=pltpu.VMEM)
+    x_parts, up_parts, down_parts, out_parts = 4, hidden // U, 2, 4
+    xs, back, mix_left, mix_right = pl.pallas_call(
+        functools.partial(routing_kernel, sections, experts, half),
+        out_shape=[
+            pltpu.VMEM((tokens, width), bf16),
+            pltpu.VMEM((2 * n, half), bf16),
+            pltpu.VMEM((tokens, 2 * n), bf16),
+            pltpu.VMEM((tokens, 2 * n), bf16),
+        ],
+        in_specs=[hbm, hbm, hbm, pl.BlockSpec(memory_space=pltpu.SMEM), hbm, hbm],
+        out_specs=[vmem] * 4,
+        scratch_shapes=[
+            pltpu.VMEM((width,), bf16),
+            pltpu.VMEM((slots, width), bf16),
+            pltpu.VMEM((tokens, padded), bf16),
+            pltpu.VMEM((tokens, 128), jnp.float32),
+            pltpu.VMEM((hidden, width), bf16),
+            pltpu.VMEM((width, hidden), bf16),
+            pltpu.VMEM((hidden, width), bf16),
+            pltpu.VMEM((2 * n, hidden), bf16),
+            pltpu.VMEM((2 * slots, half), bf16),
+            pltpu.VMEM((2 * n, half), bf16),
+            pltpu.VMEM((2 * n, half), bf16),
+            pltpu.VMEM((2 * n, half), bf16),
+            pltpu.VMEM((n - 1, 2, half), bf16),
+            pltpu.SemaphoreType.DMA((2,)),
+            pltpu.SemaphoreType.DMA((x_parts,)),
+            pltpu.SemaphoreType.DMA((up_parts,)),
+            pltpu.SemaphoreType.DMA((down_parts,)),
+            pltpu.SemaphoreType.DMA((2,)),
+            pltpu.SemaphoreType.DMA((2,)),
+            pltpu.SemaphoreType.DMA((2,)),
+        ],
+        compiler_params=pltpu.CompilerParams(
+            collective_id=0, has_side_effects=True, vmem_limit_bytes=60 * 1024 * 1024
+        ),
+    )(images, norm_gain, slot_map, logit_scale, up_weight, down_weight)
+    return pl.pallas_call(
+        functools.partial(mixing_kernel, half),
+        out_shape=jax.ShapeDtypeStruct((tokens, width), bf16),
+        in_specs=[vmem] * 4,
+        out_specs=hbm,
+        scratch_shapes=[pltpu.VMEM((tokens, width), bf16), pltpu.SemaphoreType.DMA((out_parts,))],
+    )(*(pltpu.with_memory_space_constraint(v, pltpu.VMEM) for v in (xs, back, mix_left, mix_right)))
+
+
+def general_kernel(
     sections, experts, chunk,
     x_hbm, gain_hbm, slot_hbm, scale_hbm, up_hbm, down_hbm,
     out_v,
@@ -224,9 +656,19 @@
         bf16 = jnp.bfloat16
         hbm = pl.BlockSpec(memory_space=pl.ANY)
         vmem = pl.BlockSpec(memory_space=pltpu.VMEM)
+        fits = (
+            tokens == U and slots % STRIP == 0 and experts & (experts - 1) == 0 and 2 * n <= 64
+            and half % U == 0 and 2 * half - width < U and hidden_units % (2 * U) == 0
+        )
+        if fits:
+            result = fast_call(
+                sections, experts, half, images.reshape(tokens, width), norm_gain, slot_map.T, logit_scale,
+                up_weight.reshape(hidden_units, width), down_weight.reshape(hidden_units, width),
+            )
+            return result.reshape(1, tokens, width)
         x_parts = 4
         result = pl.pallas_call(
-            functools.partial(kernel, sections, experts, chunk),
+            functools.partial(general_kernel, sections, experts, chunk),
             out_shape=pltpu.VMEM((tokens, width), bf16),
             in_specs=[hbm, hbm, hbm, pl.BlockSpec(memory_space=pltpu.HBM), hbm, hbm],
             out_specs=vmem,

time: 22.8 us -> 20.8 us (0.912)
  Pallas kernels: 21.1 us -> 20 us
  local copies, waits for them, and re-layouts: 0.86 us -> 0 us
    pallas_call x1 -> x2, Pallas kernels: 21.1 us -> 20 us  [the longest x1 18.9 us: fast_call(): pl.pallas_call(functools.partial(routing_kernel, sections, experts, half)...]
    unnamed x1 -> x0, local copies, waits for them, and re-layouts: 0.86 us -> none
where the time goes in v2:
time: 20.8 us; the launch traced here: 20.7 us
  Pallas kernels  20 us (96%)
  between operations  0.66 us (3%)
    pallas_call x1, Pallas kernels, fast_call(): pl.pallas_call(functools.partial(routing_kernel, sections, experts, half)...  18.9 us
    pallas_call x1, Pallas kernels, fast_call(): pl.pallas_call(functools.partial(mixing_kernel, half), out_shape=jax.Shap...  1.07 us

profile of v2, /device:TPU:0, one launch (start us, length us, event | category | flops | bytes accessed | tf_op | source)
XLA Modules:
  0.0 20.7 jit_solution(16578299899501455928)
XLA Ops:
  0.7 18.9 %shard_map.64 = (bf16[256,1408]{1,0:T(8,128)(2,1)S(1)}, bf16[64,768]{1,0:T(8,128)(2,1)S(1)}, bf16[256,64]{1,0:T(8,128)(2,1)S(1)}, bf16[256,64]{1,0:T(8,128)(2,1)S(1)}) custom-call(bf16[256,1408]{1,0:T(8,128)(2,1)} %bitcast.7, bf16[1408]{0:T(1024)(128)(2,1)} %gain_hbm.1, bf16[16,1408]{1,0:T(8,128)(2,1)} %bitcast.8, f32[1]{0:T(128)S(6)} %copy.7.scale_ref, ...), custom_call_target="tpu_custom_call" | custom-call | tf_op jit(solution)/shard_map/pallas_call | solution.py:419
  19.6 1.1 %shard_map.65 = bf16[256,1408]{1,0:T(8,128)(2,1)} custom-call(bf16[256,1408]{1,0:T(8,128)(2,1)S(1)} %get-tuple-element.9.xs, bf16[64,768]{1,0:T(8,128)(2,1)S(1)} %get-tuple-element.10.back, bf16[256,64]{1,0:T(8,128)(2,1)S(1)} %get-tuple-element.11.mix_left, bf16[256,64]{1,0:T(8,128)(2,1)S(1)} %get-tuple-element.12.mix_right), custom_call_target="tpu_custom_call" | custom-call | tf_op jit(solution)/shard_map/pallas_call | solution.py:455

commit v3 on v2

--- a/solution.py
+++ b/solution.py
@@ -37,6 +37,13 @@
 def gelu(x):
     k = 0.7978845608028654
     return (0.5 * x) * (1.0 + jnp.tanh(x * (k + (k * 0.044715) * (x * x))))
+
+def stage_first(upt_v, half):
+    hidden = upt_v.shape[1]
+    for t in range(2):
+        for q in range(2):
+            pltpu.matmul_push_rhs(upt_v[pl.ds(t * U, U), pl.ds(q * hidden // 2, U)], t, q)
+
 
 def expert_mlp(rows_ref, upt_v, down_v, act_v, out_ref, ups, downs, halves, half, width, lag=2):
     M = rows_ref.shape[0]
@@ -52,6 +59,7 @@
     even_strip = lax.broadcasted_iota(jnp.int32, (STRIP, U), 0) % 2 == 0
     zero = jnp.zeros((M, U), bf16)
     slot = [0, 0]
+    staged = [2, 2]
 
     def piece(s):
         return slice(s * STRIP, (s + 1) * STRIP)
@@ -59,7 +67,10 @@
     def feed(q, tile, accs, operands):
         r = slot[q]
         slot[q] = 1 - r
-        pltpu.matmul_push_rhs(tile, r, q)
+        if staged[q]:
+            staged[q] -= 1
+        else:
+            pltpu.matmul_push_rhs(tile, r, q)
         first = True
         for acc, operand in zip(accs, operands):
             for s in range(strips):
@@ -374,6 +385,7 @@
     for c in range(down_parts):
         down_copy(c).wait()
 
+    stage_first(upt_v, half)
     own1.wait()
     wait_all(recv_sem.at[0])
     expert_mlp(recv1, upt_v, down_v, act_v, send2, ups, downs, halves, half, width)
@@ -658,7 +670,7 @@
         vmem = pl.BlockSpec(memory_space=pltpu.VMEM)
         fits = (
             tokens == U and slots % STRIP == 0 and experts & (experts - 1) == 0 and 2 * n <= 64
-            and half % U == 0 and 2 * half - width < U and hidden_units % (2 * U) == 0
+            and half % U == 0 and half >= 2 * U and 2 * half - width < U and hidden_units % (2 * U) == 0
         )
         if fits:
             result = fast_call(

time: 20.8 us -> 20.7 us (level)
  no operation moved by 1% of the time
where the time goes in v3:
time: 20.7 us; the launch traced here: 20.6 us
  Pallas kernels  19.9 us (96%)
  between operations  0.66 us (3%)
    pallas_call x1, Pallas kernels, fast_call(): pl.pallas_call(functools.partial(routing_kernel, sections, experts, half)...  18.9 us
    pallas_call x1, Pallas kernels, fast_call(): pl.pallas_call(functools.partial(mixing_kernel, half), out_shape=jax.Shap...  1.08 us

profile of v3, /device:TPU:0, one launch (start us, length us, event | category | flops | bytes accessed | tf_op | source)
XLA Modules:
  0.0 20.6 jit_solution(3244448499703386260)
XLA Ops:
  0.7 18.9 %shard_map.64 = (bf16[256,1408]{1,0:T(8,128)(2,1)S(1)}, bf16[64,768]{1,0:T(8,128)(2,1)S(1)}, bf16[256,64]{1,0:T(8,128)(2,1)S(1)}, bf16[256,64]{1,0:T(8,128)(2,1)S(1)}) custom-call(bf16[256,1408]{1,0:T(8,128)(2,1)} %bitcast.7, bf16[1408]{0:T(1024)(128)(2,1)} %gain_hbm.1, bf16[16,1408]{1,0:T(8,128)(2,1)} %bitcast.8, f32[1]{0:T(128)S(6)} %copy.7.scale_ref, ...), custom_call_target="tpu_custom_call" | custom-call | tf_op jit(solution)/shard_map/pallas_call | solution.py:431
  19.5 1.1 %shard_map.65 = bf16[256,1408]{1,0:T(8,128)(2,1)} custom-call(bf16[256,1408]{1,0:T(8,128)(2,1)S(1)} %get-tuple-element.9.xs, bf16[64,768]{1,0:T(8,128)(2,1)S(1)} %get-tuple-element.10.back, bf16[256,64]{1,0:T(8,128)(2,1)S(1)} %get-tuple-element.11.mix_left, bf16[256,64]{1,0:T(8,128)(2,1)S(1)} %get-tuple-element.12.mix_right), custom_call_target="tpu_custom_call" | custom-call | tf_op jit(solution)/shard_map/pallas_call | solution.py:467
